TPU v7x, 32 devices: a whole 2x2x4 slice. The times are simulated.
32 devices in a mesh: mem: 8 (over y, x, core), pix: 4 (over z).
Axes of the slice: x: 2, y: 2, z: 4, core: 2. Of those that a mesh axis runs over, the one named last changes fastest.
Arguments:
- prior_motion: bfloat16 [64, 16, 131072], P('mem', None, 'pix'), may hold values from -6 to 6
- measured_motion: float32 [1200], replicated, may hold values from -1.6 to 1.6
- measurement_noise_stddev: float32 [1200], replicated, may hold values from 0.05 to 0.5
- gaussian_jitter: float32 [2, 1200, 64], replicated, may hold values from -6 to 6
- scene_couples: int32 [2, 1200], replicated, may hold values from 0 to 15, as said below
- targeted_tile_number: int32 [1200], replicated, may hold values from 0 to 2047
Outputs:
- analysis: bfloat16 [64, 16, 131072], P('mem', None, 'pix')
Inputs may be any that keep to these rules, and one draw needn't show every extreme that they name: scene_couples[0, k] < scene_couples[1, k]: row 0 holds the earlier acquisition, row 1 the later.
All inputs are finite; a program needn't handle non-finite values.
Results may differ from a plain program's by a relative error of at most 0.011.
Values may be sent and summed in bfloat16 or wider, within the bound.
A program may use at most 192 MiB of HBM per device.

v0:
```python
import math
import jax
import jax.numpy as jnp
from jax import lax
from jax.sharding import PartitionSpec as P

BLK = 64
PASS_COUNT = 2


def block_sums(pieces):
    part_cells = pieces.shape[2]
    block_count = part_cells // BLK
    summer = (
        jnp.arange(part_cells, dtype=jnp.int32)[:, None] // BLK
        == jnp.arange(block_count, dtype=jnp.int32)[None, :]
    ).astype(jnp.bfloat16)
    flat = jnp.dot(pieces.reshape(-1, part_cells), summer, preferred_element_type=jnp.float32)
    return flat.reshape(pieces.shape[0], pieces.shape[1], block_count)


def with_sums(pieces):
    return (pieces, block_sums(pieces))


def to_pixels(ground_motion_vector):
    return with_sums(
        lax.all_to_all(ground_motion_vector, "mem", split_axis=2, concat_axis=0, tiled=True)
    )


def to_members(pixel_state):
    return lax.all_to_all(pixel_state, "mem", split_axis=0, concat_axis=2, tiled=True)


def predict(sums, picker):
    flat_sums = sums.reshape(sums.shape[0], -1)
    return (
        jnp.dot(
            picker, flat_sums.T, precision=lax.Precision.HIGHEST, preferred_element_type=jnp.float32
        )
        / BLK
    )


def member_terms(predicted, measured_motion, member_anomaly, noise):
    realization_vectors = predicted.shape[1]
    centred = predicted - jnp.mean(predicted, axis=1, keepdims=True)
    scaled = centred / (member_anomaly[:, None] * math.sqrt(realization_vectors - 1))
    misfit = (
        measured_motion[:, None] + member_anomaly[:, None] * noise - predicted
    ) / member_anomaly[:, None]
    return (scaled, misfit)


def products(scaled, misfit):
    gram = jnp.dot(
        scaled.T, scaled, precision=lax.Precision.HIGHEST, preferred_element_type=jnp.float32
    )
    cross = jnp.dot(
        scaled.T, misfit, precision=lax.Precision.HIGHEST, preferred_element_type=jnp.float32
    )
    return (gram, cross)


def solve_mixing(gram, cross):
    realization_vectors = gram.shape[0]
    factor = jnp.linalg.cholesky(jnp.eye(realization_vectors, dtype=jnp.float32) + gram)
    return (
        jax.scipy.linalg.cho_solve((factor, True), cross) / math.sqrt(realization_vectors - 1)
    ).astype(jnp.bfloat16)


def update(pixel_state, mixing):
    realization_vectors = pixel_state.shape[0]
    average = jnp.sum(pixel_state, axis=0, dtype=jnp.float32) / realization_vectors
    anomaly = (pixel_state.astype(jnp.float32) - average).astype(jnp.bfloat16)
    change = jnp.dot(
        mixing.T, anomaly.reshape(realization_vectors, -1), preferred_element_type=jnp.float32
    )
    return (pixel_state.astype(jnp.float32) + change.reshape(pixel_state.shape)).astype(
        jnp.bfloat16
    )


def body(
    prior_motion,
    measured_motion,
    measurement_noise_stddev,
    gaussian_jitter,
    scene_couples,
    targeted_tile_number,
):
    cells_per_tile = prior_motion.shape[2]
    part_width = cells_per_tile // lax.axis_size("mem")
    local_blocks = part_width // BLK
    first_block = (
        lax.axis_index("pix") * cells_per_tile + lax.axis_index("mem") * part_width
    ) // BLK
    block_range = first_block + jnp.arange(local_blocks, dtype=jnp.int32)
    block_table = (targeted_tile_number[:, None] == block_range[None, :]).astype(jnp.float32)
    scene_timeline = jnp.arange(prior_motion.shape[1], dtype=jnp.int32)
    pair_table = (scene_timeline[None, :] == scene_couples[1][:, None]).astype(jnp.float32) - (
        scene_timeline[None, :] == scene_couples[0][:, None]
    ).astype(jnp.float32)
    picker = (pair_table[:, :, None] * block_table[:, None, :]).reshape(pair_table.shape[0], -1)
    member_anomaly = jnp.sqrt(jnp.float32(float(PASS_COUNT))) * measurement_noise_stddev
    pixel_state, sums = to_pixels(prior_motion)
    for iteration in range(PASS_COUNT):
        if iteration > 0:
            sums = block_sums(pixel_state)
        predicted = predict(sums, picker)
        predicted = lax.psum(predicted, ("mem", "pix"))
        scaled, misfit = member_terms(
            predicted, measured_motion, member_anomaly, gaussian_jitter[iteration]
        )
        gram, cross = products(scaled, misfit)
        pixel_state = update(pixel_state, solve_mixing(gram, cross))
    return to_members(pixel_state)


def solution(mesh):
    return jax.shard_map(
        body,
        mesh=mesh,
        in_specs=(P("mem", None, "pix"), P(), P(), P(), P(), P()),
        out_specs=P("mem", None, "pix"),
        check_vma=False,
    )
```

profile of v0, /device:TPU:8, one launch (start us, length us, event | category | flops | bytes accessed | tf_op | source)
XLA Modules:
  0.0 957.3 jit_solution(7385386645052010220)
XLA Ops:
  6.5 52.6 %copy.41 = bf16[8,16,32768]{1,0,2:T(8,128)(2,1)} copy(bf16[8,16,32768]{2,1,0:T(8,128)(2,1)} %param.9) | data formatting | bytes 16777216 | tf_op args[0]
  59.1 103.9 %reshape.195 = bf16[8,2,262144]{2,1,0:T(2,128)(2,1)} reshape(bf16[32768,8,16]{2,1,0:T(8,128)(2,1)} %bitcast.86) | data formatting | bytes 16777216
  171.8 90.4 %all-to-all-done = bf16[8,2,262144]{2,1,0:T(2,128)(2,1)} async-done(((bf16[8,2,262144]{2,1,0:T(2,128)(2,1)}), bf16[8,2,262144]{2,1,0:T(2,128)(2,1)}, u32[]{:S(2)}, u32[]{:S(2)}) %all-to-all-start) | async-done | bytes 8388640 | tf_op jit(solution)/shard_map/all_to_all | solution.py:28
  262.2 80.3 %reshape.196 = bf16[32768,8,16]{2,1,0:T(8,128)(2,1)} reshape(bf16[8,2,262144]{2,1,0:T(2,128)(2,1)} %all-to-all-done) | data formatting | bytes 16777216
  342.5 52.2 %copy.65 = bf16[8,16,8,4096]{3,2,1,0:T(8,128)(2,1)} copy(bf16[8,16,8,4096]{1,0,3,2:T(8,128)(2,1)} %bitcast) | data formatting | bytes 16777216 | tf_op jit(solution)/shard_map/all_to_all | solution.py:28
  394.7 11.4 %bitcast_convert_fusion = f32[8,8,16,4096]{3,0,2,1:T(8,128)} fusion(bf16[8,16,8,4096]{3,2,1,0:T(8,128)(2,1)} %copy.65), kind=kLoop, calls=%fused_computation.14 | loop fusion | flops 4194304 | bytes 25165824 | tf_op jit(solution)/shard_map/convert_element_type | solution.py:81
  406.1 5.2 fusion.8
  411.3 60.0 %copy.44 = bf16[8,8,16,4096]{3,2,1,0:T(8,128)(2,1)} copy(bf16[8,8,16,4096]{2,1,3,0:T(8,128)(2,1)} %bitcast.4) | data formatting | bytes 16777216 | tf_op jit(solution)/shard_map/all_to_all | solution.py:28
  471.3 6.5 convolution_bitcast_fusion
  478.2 6.6 convolution_multiply_fusion.1
  484.9 15.2 %copy.90 = f32[8,8,16,4096]{3,2,1,0:T(8,128)S(1)} copy(f32[8,8,16,4096]{3,0,2,1:T(8,128)} %bitcast_convert_fusion) | data formatting | bytes 33554432 | tf_op jit(solution)/shard_map/convert_element_type | solution.py:81
  500.1 10.9 %copy.73 = f32[8,8,16,4096]{3,1,2,0:T(8,128)S(1)} copy(f32[8,8,16,4096]{3,2,1,0:T(8,128)S(1)} %copy.90) | data formatting | bytes 33554432
  515.0 98.2 %all-reduce.3.cloned.1.call-done = f32[1200,64]{0,1:T(8,128)} async-done(((f32[1200,64]{0,1:T(8,128)}), f32[1200,64]{0,1:T(8,128)}) %all-reduce.3.cloned.1.call-update) | async-done | bytes 307216 | tf_op jit(solution)/shard_map/psum | solution.py:113
  615.9 5.8 cholesky.44
  630.1 21.8 %convert_reduce_fusion = (f32[16,4096]{1,0:T(8,128)S(1)}, bf16[64,16,4096]{2,0,1:T(8,128)(2,1)}) fusion(bf16[64,64,1]{1,0,2:T(8,128)(2,1)S(1)} %fusion.14, bf16[8,16,8,4096]{3,2,1,0:T(8,128)(2,1)} %bitcast.113, f32[8,8,16,4096]{3,0,2,1:T(8,128)} %bitcast_convert_fusion), kind=kOutput, calls=%fused_computation.2 | convolution fusion | flops 553582592 | bytes 33824768 | tf_op jit(solution)/shard_map/dot_general | solution.py:78
  651.9 11.4 %copy.51 = bf16[64,16,4096]{2,1,0:T(8,128)(2,1)} copy(bf16[64,16,4096]{2,0,1:T(8,128)(2,1)} %get-tuple-element.12) | data formatting | bytes 16777216 | tf_op jit(solution)/shard_map/convert_element_type | solution.py:81
  663.2 5.8 fusion.9
  669.2 6.6 convolution_multiply_fusion
  675.9 128.1 %all-reduce.5.cloned.1.call-done = f32[1200,64]{0,1:T(8,128)} async-done(((f32[1200,64]{0,1:T(8,128)}), f32[1200,64]{0,1:T(8,128)}) %all-reduce.5.cloned.1.call-update) | async-done | bytes 307216 | tf_op jit(solution)/shard_map/psum | solution.py:113
  806.6 5.8 cholesky.55
  820.8 10.6 %fusion.1 = bf16[64,16,4096]{2,0,1:T(8,128)(2,1)} fusion(bf16[64,16,4096]{2,0,1:T(8,128)(2,1)} %get-tuple-element.12, bf16[64,64,1]{1,0,2:T(8,128)(2,1)S(1)} %fusion.13, f32[16,4096]{1,0:T(8,128)S(1)} %broadcast_multiply_fusion.1), kind=kOutput, calls=%fused_computation.4 | convolution fusion | flops 562036736 | bytes 17047552 | tf_op jit(solution)/shard_map/dot_general | solution.py:78
  831.4 11.2 %copy.58 = bf16[64,16,4096]{2,1,0:T(8,128)(2,1)} copy(bf16[64,16,4096]{2,0,1:T(8,128)(2,1)} %fusion.1) | data formatting | bytes 16777216 | tf_op jit(solution)/shard_map/convert_element_type | solution.py:81
  842.6 99.7 %all_to_all.33 = bf16[64,16,4096]{2,1,0:T(8,128)(2,1)} all-to-all(bf16[64,16,4096]{2,1,0:T(8,128)(2,1)} %copy.58), channel_id=1, replica_groups=mesh['mem'=8,'pix'=4] {'mem'}, dimensions={0} | all-to-all | bytes 16777216 | tf_op jit(solution)/shard_map/all_to_all | solution.py:33
  942.3 7.9 copy.72
  (53 shorter events, 35.0 us)
Async XLA Ops:
  163.1 5.7 copy-start
  163.1 5.7 copy-start.1
  163.1 5.7 copy-start.2
  163.1 99.1 %all-to-all-start = ((bf16[8,2,262144]{2,1,0:T(2,128)(2,1)}), bf16[8,2,262144]{2,1,0:T(2,128)(2,1)}, u32[]{:S(2)}, u32[]{:S(2)}) async-start(bf16[8,2,262144]{2,1,0:T(2,128)(2,1)} %reshape.195), calls=%async_computation | async-start | bytes 16777216 | tf_op jit(solution)/shard_map/all_to_all | solution.py:28
  168.2 445.1 %all-reduce.3.cloned.1.call-start = ((), (), s32[]{:S(2)}) async-start(), calls=%async_computation.2 | async-start | bytes 655360 | tf_op jit(solution)/shard_map/psum | solution.py:113
  484.9 319.1 %all-reduce.5.cloned.1.call-start = ((), (), s32[]{:S(2)}) async-start(), calls=%async_computation.3 | async-start | bytes 655360 | tf_op jit(solution)/shard_map/psum | solution.py:113
  511.1 117.0 %copy-start.3 = (f32[2,1200,64]{1,2,0:T(8,128)S(1)}, f32[2,1200,64]{1,2,0:T(8,128)}, u32[]{:S(2)}) copy-start(f32[2,1200,64]{1,2,0:T(8,128)} %param.12) | copy-start | bytes 1843204
  511.1 117.0 %copy-start.4 = (f32[1200]{0:T(1024)S(1)}, f32[1200]{0:T(1024)}, u32[]{:S(2)}) copy-start(f32[1200]{0:T(1024)} %param.10) | copy-start | bytes 14404
Sparse Core Ops, SparseCore 0:
  485.0 128.2 all-reduce.2
  676.0 127.9 all-reduce.4
where the time goes:
time: 970 us; the launch traced here: 957 us
  local copies, waits for them, and re-layouts  406 us (42%)
  waiting for transfers between devices  317 us (33%)
  blocking collectives  99.7 us (10%)
  matrix products  64.9 us (7%)
  other arithmetic  49.9 us (5%)
  between operations  13.9 us (1%)
    unnamed x15, local copies, waits for them, and re-layouts  248 us
    psum x2, waiting for transfers between devices, body(): predicted = lax.psum(predicted, ('mem', 'pix'))  226 us
    all_to_all x2, local copies, waits for them, and re-layouts, to_pixels(): lax.all_to_all(ground_motion_vector, 'mem', split_axis=2, concat_axis=0,...  112 us
    all_to_all x1, blocking collectives, to_members(): lax.all_to_all(pixel_state, 'mem', split_axis=0, concat_axis=2, tiled=True)  99.7 us
    all_to_all x1, waiting for transfers between devices, to_pixels(): lax.all_to_all(ground_motion_vector, 'mem', split_axis=2, concat_axis=0,...  90.4 us
    dot_general x2, matrix products, update(): jnp.dot(mixing.T, anomaly.reshape(realization_vectors, -1), preferred_ele...  32.4 us
    convert_element_type x2, local copies, waits for them, and re-layouts, update(): (pixel_state.astype(jnp.float32) + change.reshape(pixel_state.shape)).ast...  22.6 us
  transfers between devices with their start and end apart: 3, of which 3 were waited for; matrix products, arithmetic and copies ran while one was open for 3% of the time, Pallas kernels for 0%

commit v1 on v0

--- a/solution.py
+++ b/solution.py
@@ -1,3 +1,4 @@
+import functools
 import math
 import jax
 import jax.numpy as jnp
@@ -6,6 +7,18 @@
 
 BLK = 64
 PASS_COUNT = 2
+
+
+def do_ticks(content, mesh_dim, dim_no, where_dim):
+    return jnp.concatenate(
+        lax.all_to_all(
+            jnp.stack(jnp.split(content, lax.axis_size(mesh_dim), dim_no), 0), mesh_dim, 0, 0
+        ),
+        where_dim,
+    )
+
+
+cube_order = functools.partial(do_ticks, mesh_dim="mem", dim_no=2, where_dim=0)
 
 
 def block_sums(pieces):
@@ -24,9 +37,7 @@
 
 
 def to_pixels(ground_motion_vector):
-    return with_sums(
-        lax.all_to_all(ground_motion_vector, "mem", split_axis=2, concat_axis=0, tiled=True)
-    )
+    return with_sums(cube_order(ground_motion_vector))
 
 
 def to_members(pixel_state):

time: 970 us -> 621 us (0.64)
  local copies, waits for them, and re-layouts: 406 us -> 60.2 us
    unnamed x15 -> x19, local copies, waits for them, and re-layouts: 248 us -> 26.9 us
    all_to_all x2 -> x0, local copies, waits for them, and re-layouts: 112 us -> none  [to_pixels(): lax.all_to_all(ground_motion_vector, 'mem', split_axis=2, concat_axis=0,...]
    convert_element_type x1 -> x0, local copies, waits for them, and re-layouts: 15.2 us -> none  [update(): pixel_state.astype(jnp.float32) + change.reshape(pixel_state.shape)]
    convert_element_type x1 -> x0, other arithmetic: 11.4 us -> none  [update(): pixel_state.astype(jnp.float32) + change.reshape(pixel_state.shape)]
    unnamed x1 -> x2, other arithmetic: 0.02 us -> 10.9 us
  transfers between devices with their start and end apart: 3 -> 3, of which waited for: 3 -> 3; matrix products, arithmetic and copies ran while one was open for 3% -> 5% of each run, Pallas kernels for 0% -> 0%
where the time goes in v1:
time: 621 us; the launch traced here: 614 us
  waiting for transfers between devices  321 us (52%)
  blocking collectives  99.7 us (16%)
  matrix products  64 us (10%)
  local copies, waits for them, and re-layouts  60.2 us (10%)
  other arithmetic  48.9 us (8%)
  between operations  13.9 us (2%)
    psum x2, waiting for transfers between devices, body(): predicted = lax.psum(predicted, ('mem', 'pix'))  230 us
    all_to_all x1, blocking collectives, to_members(): lax.all_to_all(pixel_state, 'mem', split_axis=0, concat_axis=2, tiled=True)  99.7 us
    all_to_all x1, waiting for transfers between devices, do_ticks(): lax.all_to_all(jnp.stack(jnp.split(content, lax.axis_size(mesh_dim), dim_...  90.9 us
    dot_general x2, matrix products, update(): jnp.dot(mixing.T, anomaly.reshape(realization_vectors, -1), preferred_ele...  32.2 us
    unnamed x19, local copies, waits for them, and re-layouts  26.9 us
    convert_element_type x2, local copies, waits for them, and re-layouts, update(): (pixel_state.astype(jnp.float32) + change.reshape(pixel_state.shape)).ast...  22.6 us
    dot_general x2, matrix products, predict(): jnp.dot(picker, flat_sums.T, precision=lax.Precision.HIGHEST, preferred_e...  13.3 us
    another operation x6, other arithmetic, solve_mixing(): jnp.linalg.cholesky(jnp.eye(realization_vectors, dtype=jnp.float32) + gram)  13 us
  transfers between devices with their start and end apart: 3, of which 3 were waited for; matrix products, arithmetic and copies ran while one was open for 5% of the time, Pallas kernels for 0%

profile of v1, /device:TPU:8, one launch (start us, length us, event | category | flops | bytes accessed | tf_op | source)
XLA Modules:
  0.0 613.6 jit_solution(8426941856511718304)
XLA Ops:
  11.1 2.3 bitcast_dynamic-update-slice_fusion.5
  24.8 5.1 all-to-all-start
  30.2 2.9 broadcast_multiply_fusion
  33.1 90.9 %all-to-all-done = bf16[8,8,16,4096]{3,2,1,0:T(8,128)(2,1)} async-done(((bf16[8,8,16,4096]{3,2,1,0:T(8,128)(2,1)}), bf16[8,8,16,4096]{3,2,1,0:T(8,128)(2,1)}, u32[]{:S(2)}, u32[]{:S(2)}) %all-to-all-start) | async-done | bytes 8388640 | tf_op jit(solution)/shard_map/all_to_all | solution.py:14
  124.0 4.8 convert_reduce_fusion.1
  128.9 5.8 fusion.9
  134.9 6.6 %convolution_multiply_fusion.1 = f32[1200,64]{0,1:T(8,128)} fusion(f32[1200,1024]{0,1:T(8,128)} %bitcast.114, f32[64,1024]{1,0:T(8,128)S(1)} %reshape_reshape.10), kind=kOutput, calls=%fused_computation.17 | convolution fusion | flops 943795200 | bytes 5484544 | tf_op jit(solution)/shard_map/dot_general | solution.py:50
  142.1 10.9 %convert_bitcast_fusion = (f32[8,8,16,4096]{3,2,1,0:T(8,128)S(1)}, f32[8,8,16,4096]{3,2,1,0:T(8,128)}) fusion(bf16[8,8,16,4096]{3,2,1,0:T(8,128)(2,1)} %all-to-all-done), kind=kLoop, calls=%fused_computation.14 | loop fusion | flops 4194304 | bytes 41943040
  153.0 10.8 %copy.52 = f32[8,8,16,4096]{3,1,2,0:T(8,128)S(1)} copy(f32[8,8,16,4096]{3,2,1,0:T(8,128)S(1)} %get-tuple-element.9) | data formatting | bytes 33554432
  163.8 3.9 subtract_convert_fusion
  167.7 102.2 %all-reduce.3.cloned.1.call-done = f32[1200,64]{0,1:T(8,128)} async-done(((f32[1200,64]{0,1:T(8,128)}), f32[1200,64]{0,1:T(8,128)}) %all-reduce.3.cloned.1.call-update) | async-done | bytes 307216 | tf_op jit(solution)/shard_map/psum | solution.py:124
  272.5 5.8 cholesky.44
  279.6 4.9 custom-call.8
  286.5 21.6 %convert_reduce_fusion = (f32[16,4096]{1,0:T(8,128)S(1)}, bf16[64,16,4096]{2,0,1:T(8,128)(2,1)}) fusion(bf16[64,64,1]{1,0,2:T(8,128)(2,1)S(1)} %fusion.13, bf16[8,16,8,4096]{3,2,1,0:T(8,128)(2,1)} %bitcast.116, f32[8,8,16,4096]{3,2,1,0:T(8,128)} %get-tuple-element.10), kind=kOutput, calls=%fused_computation.2 | convolution fusion | flops 553582592 | bytes 33824768 | tf_op jit(solution)/shard_map/dot_general | solution.py:89
  308.1 11.4 %copy.31 = bf16[64,16,4096]{2,1,0:T(8,128)(2,1)} copy(bf16[64,16,4096]{2,0,1:T(8,128)(2,1)} %get-tuple-element.14) | data formatting | bytes 16777216 | tf_op jit(solution)/shard_map/convert_element_type | solution.py:92
  319.5 5.8 fusion.8
  325.5 6.6 %convolution_multiply_fusion = f32[1200,64]{0,1:T(8,128)} fusion(f32[1200,1024]{0,1:T(8,128)} %bitcast.115, f32[64,1024]{1,0:T(8,128)S(1)} %reshape_reshape.11), kind=kOutput, calls=%fused_computation.16 | convolution fusion | flops 943795200 | bytes 5484544 | tf_op jit(solution)/shard_map/dot_general | solution.py:50
  332.1 128.1 %all-reduce.5.cloned.1.call-done = f32[1200,64]{0,1:T(8,128)} async-done(((f32[1200,64]{0,1:T(8,128)}), f32[1200,64]{0,1:T(8,128)}) %all-reduce.5.cloned.1.call-update) | async-done | bytes 307216 | tf_op jit(solution)/shard_map/psum | solution.py:124
  462.9 5.8 cholesky.55
  470.1 5.0 custom-call.9
  477.1 10.6 %fusion.1 = bf16[64,16,4096]{2,0,1:T(8,128)(2,1)} fusion(bf16[64,16,4096]{2,0,1:T(8,128)(2,1)} %get-tuple-element.14, bf16[64,64,1]{1,0,2:T(8,128)(2,1)S(1)} %fusion.12, f32[16,4096]{1,0:T(8,128)S(1)} %broadcast_multiply_fusion.1), kind=kOutput, calls=%fused_computation.4 | convolution fusion | flops 562036736 | bytes 17047552 | tf_op jit(solution)/shard_map/dot_general | solution.py:89
  487.7 11.2 %copy.38 = bf16[64,16,4096]{2,1,0:T(8,128)(2,1)} copy(bf16[64,16,4096]{2,0,1:T(8,128)(2,1)} %fusion.1) | data formatting | bytes 16777216 | tf_op jit(solution)/shard_map/convert_element_type | solution.py:92
  498.9 99.7 %all_to_all.23 = bf16[64,16,4096]{2,1,0:T(8,128)(2,1)} all-to-all(bf16[64,16,4096]{2,1,0:T(8,128)(2,1)} %copy.38), channel_id=1, replica_groups=mesh['mem'=8,'pix'=4] {'mem'}, dimensions={0} | all-to-all | bytes 16777216 | tf_op jit(solution)/shard_map/all_to_all | solution.py:44
  598.7 7.9 %copy.51 = bf16[8,8,2,8,4096]{4,3,0,2,1:T(8,128)(2,1)} copy(bf16[8,8,2,8,4096]{4,3,2,1,0:T(8,128)(2,1)} %bitcast.117) | data formatting | bytes 16777216 | tf_op jit(solution)/shard_map/all_to_all | solution.py:44
  (54 shorter events, 28.9 us)
Async XLA Ops:
  24.8 5.2 copy-start
  24.8 5.2 copy-start.1
  24.8 5.3 copy-start.2
  24.8 99.1 %all-to-all-start = ((bf16[8,8,16,4096]{3,2,1,0:T(8,128)(2,1)}), bf16[8,8,16,4096]{3,2,1,0:T(8,128)(2,1)}, u32[]{:S(2)}, u32[]{:S(2)}) async-start(bf16[8,8,16,4096]{3,2,1,0:T(8,128)(2,1)} %bitcast_dynamic-update-slice_fusion), calls=%async_computation | async-start | bytes 16777216 | tf_op jit(solution)/shard_map/all_to_all | solution.py:14
  29.9 239.9 %all-reduce.3.cloned.1.call-start = ((), (), s32[]{:S(2)}) async-start(), calls=%async_computation.2 | async-start | bytes 655360 | tf_op jit(solution)/shard_map/psum | solution.py:124
  141.6 318.7 %all-reduce.5.cloned.1.call-start = ((), (), s32[]{:S(2)}) async-start(), calls=%async_computation.3 | async-start | bytes 655360 | tf_op jit(solution)/shard_map/psum | solution.py:124
  163.8 120.7 %copy-start.3 = (f32[2,1200,64]{1,2,0:T(8,128)S(1)}, f32[2,1200,64]{1,2,0:T(8,128)}, u32[]{:S(2)}) copy-start(f32[2,1200,64]{1,2,0:T(8,128)} %param.12) | copy-start | bytes 1843204
  163.8 120.7 %copy-start.4 = (f32[1200]{0:T(1024)S(1)}, f32[1200]{0:T(1024)}, u32[]{:S(2)}) copy-start(f32[1200]{0:T(1024)} %param.10) | copy-start | bytes 14404
Sparse Core Ops, SparseCore 0:
  141.7 128.1 all-reduce.2
  332.2 127.9 all-reduce.4
